TPU v7x, 32 devices: a whole 2x2x4 slice. The times are simulated.
32 devices in a mesh: clip: 4 (over y, x), head: 8 (over z, core).
Axes of the slice: x: 2, y: 2, z: 4, core: 2. Of those that a mesh axis runs over, the one named last changes fastest.
Arguments:
- queries: bfloat16 [8192, 4096], P(('clip', 'head')), may hold values from -6 to 6
- key_rows: bfloat16 [8192, 4096], P(('clip', 'head')), may hold values from -6 to 6
- value_rows: bfloat16 [8192, 4096], P(('clip', 'head')), may hold values from -6 to 6
- query_tangent: bfloat16 [8192, 4096], P(('clip', 'head')), may hold values from -6 to 6
- key_tangent: bfloat16 [8192, 4096], P(('clip', 'head')), may hold values from -6 to 6
- value_tangent: bfloat16 [8192, 4096], P(('clip', 'head')), may hold values from -6 to 6
- partners: int32 [8, 2], replicated, may hold values from 0 to 7, as said below
- cotangent: bfloat16 [8192, 3072], P('clip'), may hold values from -6 to 6
Outputs:
- attended: bfloat16 [8192, 4096], P(('clip', 'head'))
- attended_tangent: bfloat16 [8192, 4096], P(('clip', 'head'))
- weight_grad: float32 [3072, 4096], P('clip', 'head')
Inputs may be any that keep to these rules, and one draw needn't show every extreme that they name: `partners`: for clip c the two entries are distinct clips (c - d) mod 8 with 1 <= d <= 2 + c % 2.
All inputs are finite; a program needn't handle non-finite values.
Results may differ from a plain program's by a relative error of at most 0.0051.
Values may be sent and summed in bfloat16 or wider, within the bound.
A program may use at most 192 MiB of HBM per device.

v0:
```python
import jax
import jax.numpy as jnp
from jax import lax
from jax.sharding import PartitionSpec as P

HDIM = 128
CLIP = 1024


def shifted(shard, axis, by):
    length = lax.axis_size(axis)
    return lax.ppermute(shard, axis, [(i, (i + by) % length) for i in range(length)])


def as_sent(shard):
    return jax.tree.map(lambda a: a.astype(jnp.bfloat16) if a.dtype == jnp.float32 else a, shard)


def attend_block(query_block, qtan_block, key_win, value_win, ktan_win, vtan_win):
    score_scale = query_block.shape[-1] ** (-0.5)
    scores = (
        jnp.einsum("qhd,khd->hqk", query_block, key_win, preferred_element_type=jnp.float32)
        * score_scale
    )
    score_tan = (
        jnp.einsum("qhd,khd->hqk", qtan_block, key_win, preferred_element_type=jnp.float32)
        + jnp.einsum("qhd,khd->hqk", query_block, ktan_win, preferred_element_type=jnp.float32)
    ) * score_scale
    row_max = jnp.max(scores, axis=-1, keepdims=True)
    raw_weights = jnp.exp(scores - row_max)
    row_total = jnp.sum(raw_weights, axis=-1, keepdims=True)
    probability = raw_weights / row_total
    tangent_mean = jnp.sum(probability * score_tan, axis=-1, keepdims=True)
    prob_tangent = probability * (score_tan - tangent_mean)
    prob_low = probability.astype(jnp.bfloat16)
    tangent_low = prob_tangent.astype(jnp.bfloat16)
    result_out = jnp.einsum("hqk,khd->qhd", prob_low, value_win, preferred_element_type=jnp.float32)
    tangent_out = jnp.einsum(
        "hqk,khd->qhd", tangent_low, value_win, preferred_element_type=jnp.float32
    ) + jnp.einsum("hqk,khd->qhd", prob_low, vtan_win, preferred_element_type=jnp.float32)
    return (result_out.astype(jnp.bfloat16), tangent_out.astype(jnp.bfloat16))


def on_device(
    queries, key_rows, value_rows, query_tangent, key_tangent, value_tangent, partners, cotangent
):
    clip_count = lax.axis_size("clip")
    regrouped = (
        lax.all_to_all(queries, "head", split_axis=1, concat_axis=0, tiled=True),
        lax.all_to_all(key_rows, "head", split_axis=1, concat_axis=0, tiled=True),
        lax.all_to_all(value_rows, "head", split_axis=1, concat_axis=0, tiled=True),
        lax.all_to_all(query_tangent, "head", split_axis=1, concat_axis=0, tiled=True),
        lax.all_to_all(key_tangent, "head", split_axis=1, concat_axis=0, tiled=True),
        lax.all_to_all(value_tangent, "head", split_axis=1, concat_axis=0, tiled=True),
    )
    query_h, key_h, value_h, qtan_h, ktan_h, vtan_h = regrouped
    prev_key, prev_value, prev_ktan, prev_vtan = shifted(
        (key_h, value_h, ktan_h, vtan_h), "clip", 1
    )
    window_key = jnp.concatenate([prev_key, key_h], axis=0)
    window_value = jnp.concatenate([prev_value, value_h], axis=0)
    window_ktan = jnp.concatenate([prev_ktan, ktan_h], axis=0)
    window_vtan = jnp.concatenate([prev_vtan, vtan_h], axis=0)
    group_rows = query_h.shape[0]
    cols_here = query_h.shape[1]
    heads_here = cols_here // HDIM
    clips_here = group_rows // CLIP
    total_clips = clips_here * clip_count
    first_clip = lax.axis_index("clip") * clips_here
    block_rows = min(512, CLIP)

    def one_clip(within):
        partner_row = lax.dynamic_slice_in_dim(partners, first_clip + within, 1, 0)[0]
        slots_here = (partner_row - first_clip + clips_here) % total_clips
        slot_list = [clips_here + within, slots_here[0], slots_here[1]]

        def window(array):
            parts = [lax.dynamic_slice_in_dim(array, slot * CLIP, CLIP, 0) for slot in slot_list]
            return jnp.concatenate(parts, axis=0).reshape(3 * CLIP, heads_here, HDIM)

        key_win = window(window_key)
        value_win = window(window_value)
        ktan_win = window(window_ktan)
        vtan_win = window(window_vtan)
        clip_start = within * CLIP
        query_clip = lax.dynamic_slice_in_dim(query_h, clip_start, CLIP, 0).reshape(
            CLIP, heads_here, HDIM
        )
        qtan_clip = lax.dynamic_slice_in_dim(qtan_h, clip_start, CLIP, 0).reshape(
            CLIP, heads_here, HDIM
        )
        outputs = []
        tangents = []
        for block in range(CLIP // block_rows):
            lower = block * block_rows
            result_out, tangent_out = attend_block(
                query_clip[lower : lower + block_rows],
                qtan_clip[lower : lower + block_rows],
                key_win,
                value_win,
                ktan_win,
                vtan_win,
            )
            outputs.append(result_out.reshape(block_rows, cols_here))
            tangents.append(tangent_out.reshape(block_rows, cols_here))
        return (jnp.concatenate(outputs, axis=0), jnp.concatenate(tangents, axis=0))

    results = lax.map(one_clip, jnp.arange(clips_here, dtype=jnp.int32))
    output_h = results[0].reshape(group_rows, cols_here)
    tangent_h = results[1].reshape(group_rows, cols_here)
    attended, attended_tangent = (
        lax.all_to_all(as_sent(output_h), "head", split_axis=0, concat_axis=1, tiled=True).astype(
            output_h.dtype
        ),
        lax.all_to_all(as_sent(tangent_h), "head", split_axis=0, concat_axis=1, tiled=True).astype(
            tangent_h.dtype
        ),
    )
    partial_term = lax.dot_general(
        cotangent, output_h, (((0,), (0,)), ((), ())), preferred_element_type=jnp.float32
    )
    weight_grad = lax.psum_scatter(partial_term, "clip", scatter_dimension=0, tiled=True)
    return (attended, attended_tangent, weight_grad)


def solution(mesh):
    return jax.shard_map(
        on_device,
        mesh=mesh,
        in_specs=(
            P(("clip", "head"), None),
            P(("clip", "head"), None),
            P(("clip", "head"), None),
            P(("clip", "head"), None),
            P(("clip", "head"), None),
            P(("clip", "head"), None),
            P(),
            P("clip", None),
        ),
        out_specs=(P(("clip", "head"), None), P(("clip", "head"), None), P("clip", "head")),
        check_vma=False,
    )
```

profile of v0, /device:TPU:0, one launch (start us, length us, event | category | flops | bytes accessed | tf_op | source)
XLA Modules:
  0.0 1080.0 jit_solution(4664718953220969203)
XLA Ops:
  21.7 45.0 %all-to-all-done.2 = bf16[256,8,512]{0,2,1:T(8,128)(2,1)S(1)} async-done(((bf16[256,8,512]{0,2,1:T(8,128)(2,1)}), bf16[256,8,512]{0,2,1:T(8,128)(2,1)S(1)}, u32[]{:S(2)}, u32[]{:S(2)}) %all-to-all-start.2) | async-done | bytes 2097184 | tf_op jit(solution)/shard_map/all_to_all | solution.py:50
  75.1 44.9 %all-to-all-done.4 = bf16[256,8,512]{0,2,1:T(8,128)(2,1)} async-done(((bf16[256,8,512]{0,2,1:T(8,128)(2,1)}), bf16[256,8,512]{0,2,1:T(8,128)(2,1)}, u32[]{:S(2)}, u32[]{:S(2)}) %all-to-all-start.4) | async-done | bytes 2097184 | tf_op jit(solution)/shard_map/all_to_all | solution.py:53
  128.5 45.0 %all-to-all-done.5 = bf16[256,8,512]{0,2,1:T(8,128)(2,1)} async-done(((bf16[256,8,512]{0,2,1:T(8,128)(2,1)}), bf16[256,8,512]{0,2,1:T(8,128)(2,1)}, u32[]{:S(2)}, u32[]{:S(2)}) %all-to-all-start.5) | async-done | bytes 2097184 | tf_op jit(solution)/shard_map/all_to_all | solution.py:54
  181.9 45.0 %all-to-all-done = bf16[256,8,512]{0,2,1:T(8,128)(2,1)} async-done(((bf16[256,8,512]{0,2,1:T(8,128)(2,1)}), bf16[256,8,512]{0,2,1:T(8,128)(2,1)}, u32[]{:S(2)}, u32[]{:S(2)}) %all-to-all-start) | async-done | bytes 2097184 | tf_op jit(solution)/shard_map/all_to_all | solution.py:51
  235.3 44.9 %all-to-all-done.1 = bf16[256,8,512]{0,2,1:T(8,128)(2,1)} async-done(((bf16[256,8,512]{0,2,1:T(8,128)(2,1)}), bf16[256,8,512]{0,2,1:T(8,128)(2,1)}, u32[]{:S(2)}, u32[]{:S(2)}) %all-to-all-start.1) | async-done | bytes 2097184 | tf_op jit(solution)/shard_map/all_to_all | solution.py:49
  306.8 26.8 %all-to-all-done.3 = bf16[256,8,512]{0,2,1:T(8,128)(2,1)} async-done(((bf16[256,8,512]{0,2,1:T(8,128)(2,1)}), bf16[256,8,512]{0,2,1:T(8,128)(2,1)}, u32[]{:S(2)}, u32[]{:S(2)}) %all-to-all-start.3) | async-done | bytes 2097184 | tf_op jit(solution)/shard_map/all_to_all | solution.py:52
  348.4 33.3 %collective-permute-done.2 = bf16[2048,512]{1,0:T(8,128)(2,1)} collective-permute-done((bf16[2048,512]{1,0:T(8,128)(2,1)}, bf16[2048,512]{1,0:T(8,128)(2,1)}, u32[]{:S(2)}, u32[]{:S(2)}) %collective-permute-start.2) | collective-permute-done | bytes 2097184 | tf_op jit(solution)/shard_map/ppermute | solution.py:12
  392.6 34.1 %collective-permute-done.3 = bf16[2048,512]{1,0:T(8,128)(2,1)} collective-permute-done((bf16[2048,512]{1,0:T(8,128)(2,1)}, bf16[2048,512]{1,0:T(8,128)(2,1)}, u32[]{:S(2)}, u32[]{:S(2)}) %collective-permute-start.3) | collective-permute-done | bytes 2097184 | tf_op jit(solution)/shard_map/ppermute | solution.py:12
  437.5 33.5 %collective-permute-done = bf16[2048,512]{1,0:T(8,128)(2,1)} collective-permute-done((bf16[2048,512]{1,0:T(8,128)(2,1)S(1)}, bf16[2048,512]{1,0:T(8,128)(2,1)}, u32[]{:S(2)}, u32[]{:S(2)}) %collective-permute-start) | collective-permute-done | bytes 2097184 | tf_op jit(solution)/shard_map/ppermute | solution.py:12
  481.8 461.5 %while.14 = (s32[]{:T(128)}, bf16[2,1024,512]{2,1,0:T(8,128)(2,1)}, bf16[2,1024,512]{2,1,0:T(8,128)(2,1)}, s32[2]{0:T(128)}, bf16[4096,512]{0,1:T(8,128)(2,1)}, ...) while((s32[]{:T(128)}, bf16[2,1024,512]{2,1,0:T(8,128)(2,1)}, ...), condition=%wide.region_7.8_spmd, body=%wide.region_0.7_spmd.sunk | while | flops 19572197376 | bytes 686934336 | solution.py:108
  517.1 13.8 %fusion.128 = (f32[4,512]{1,0:T(4,128)S(1)}, f32[4,512,3072]{2,1,0:T(8,128)}) fusion(bf16[512,4,128]{0,2,1:T(8,128)(2,1)} %bitcast.174, bf16[3072,4,128]{0,2,1:T(8,128)(2,1)S(1)} %bitcast.158), kind=kOutput, calls=%fused_computation.78.clone.1 | convolution fusion | flops 1629490176 | bytes 28844032 | tf_op jit(solution)/shard_map/while/body/eval_jaxpr/sub | solution.py:30
  533.0 11.3 %fusion.134 = f32[4,512,3072]{2,1,0:T(8,128)} fusion(bf16[512,4,128]{0,2,1:T(8,128)(2,1)} %bitcast.170, bf16[3072,4,128]{0,2,1:T(8,128)(2,1)S(1)} %bitcast.159), kind=kOutput, calls=%fused_computation.79.clone.1 | convolution fusion | flops 1610612736 | bytes 28835840 | tf_op jit(solution)/shard_map/while/body/eval_jaxpr/qhd,khd->hqk/dot_general | solution.py:26
  548.2 28.1 %multiply_reduce_fusion.7 = (f32[4,512]{1,0:T(4,128)S(1)}, f32[4,512,3072]{2,1,0:T(8,128)}) fusion(f32[4,512,3072]{2,1,0:T(8,128)} %get-tuple-element.400, f32[4,512]{1,0:T(4,128)S(1)} %get-tuple-element.401, f32[4,512,3072]{2,1,0:T(8,128)} %fusion.134, bf16[512,4,128]{0,2,1:T(8,128)(2,1)} %bitcast.175, bf16[3072,4,128]{0,2,1:T(8,128)(2,1)} %bitcast.166), kind=kOutput, calls=%fused_computation.6.clone.1 | convolution fusion | flops 1642067968 | bytes 79183872 | tf_op jit(solution)/shard_map/while/body/eval_jaxpr/qhd,khd->hqk/dot_general | solution.py:27
  578.3 12.7 %fusion.133 = f32[4,128,512]{2,1,0:T(8,128)} fusion(bf16[3072,4,128]{0,2,1:T(8,128)(2,1)S(1)} %bitcast.168, f32[4,512,3072]{2,1,0:T(8,128)} %get-tuple-element.400, f32[4,512]{1,0:T(4,128)S(1)} %get-tuple-element.401), kind=kOutput, calls=%fused_computation.26.clone.1 | convolution fusion | flops 1623195648 | bytes 29368320 | tf_op jit(solution)/shard_map/while/body/eval_jaxpr/hqk,khd->qhd/dot_general | solution.py:40
  592.3 18.7 %fusion.135 = bf16[4,128,512]{2,1,0:T(8,128)(2,1)} fusion(f32[4,128,512]{2,1,0:T(8,128)S(1)} %copy-done.15, bf16[3072,4,128]{0,2,1:T(8,128)(2,1)S(1)} %bitcast.162, f32[4,512,3072]{2,1,0:T(8,128)} %get-tuple-element.412, f32[4,512]{1,0:T(4,128)S(1)} %get-tuple-element.413, f32[4,512,3072]{2,1,0:T(8,128)} %get-tuple-element.400, ...), kind=kOutput, calls=%fused_computation.40.clone.1 | convolution fusion | flops 1636302848 | bytes 55066624 | tf_op jit(solution)/shard_map/while/body/eval_jaxpr/hqk,khd->qhd/dot_general | solution.py:38
  626.4 13.7 %fusion.126 = (f32[4,512]{1,0:T(4,128)S(1)}, f32[4,512,3072]{2,1,0:T(8,128)}) fusion(bf16[512,4,128]{0,2,1:T(8,128)(2,1)} %bitcast.176, bf16[3072,4,128]{0,2,1:T(8,128)(2,1)S(1)} %bitcast.161), kind=kOutput, calls=%fused_computation.77.clone.1 | convolution fusion | flops 1629490176 | bytes 28844032 | tf_op jit(solution)/shard_map/while/body/eval_jaxpr/sub | solution.py:30
  640.1 28.2 %multiply_reduce_fusion.6 = (f32[4,512]{1,0:T(4,128)S(1)}, f32[4,512,3072]{2,1,0:T(8,128)}) fusion(f32[4,512,3072]{2,1,0:T(8,128)} %get-tuple-element.397, f32[4,512]{1,0:T(4,128)S(1)} %get-tuple-element.398, f32[4,512,3072]{2,1,0:T(8,128)} %fusion.131, bf16[512,4,128]{0,2,1:T(8,128)(2,1)} %bitcast.177, bf16[3072,4,128]{0,2,1:T(8,128)(2,1)} %bitcast.167), kind=kOutput, calls=%fused_computation.3.clone.1 | convolution fusion | flops 1642067968 | bytes 79183872 | tf_op jit(solution)/shard_map/while/body/eval_jaxpr/qhd,khd->hqk/dot_general | solution.py:27
  678.9 17.9 %fusion.132 = bf16[4,128,512]{2,1,0:T(8,128)(2,1)S(1)} fusion(f32[4,128,512]{2,1,0:T(8,128)S(1)} %fusion.130, bf16[3072,4,128]{0,2,1:T(8,128)(2,1)S(1)} %bitcast.164, f32[4,512,3072]{2,1,0:T(8,128)} %get-tuple-element.409, f32[4,512]{1,0:T(4,128)S(1)} %get-tuple-element.410, f32[4,512,3072]{2,1,0:T(8,128)} %get-tuple-element.397, ...), kind=kOutput, calls=%fused_computation.41.clone.1 | convolution fusion | flops 1636302848 | bytes 55066624 | tf_op jit(solution)/shard_map/while/body/eval_jaxpr/hqk,khd->qhd/dot_general | solution.py:38
  698.6 11.6 %fusion.129 = bf16[4,128,512]{2,1,0:T(8,128)(2,1)S(1)} fusion(bf16[3072,4,128]{0,2,1:T(8,128)(2,1)} %bitcast.163, f32[4,512,3072]{2,1,0:T(8,128)} %get-tuple-element.400, f32[4,512]{1,0:T(4,128)S(1)} %get-tuple-element.401), kind=kOutput, calls=%fused_computation.38.clone.1 | convolution fusion | flops 1623457792 | bytes 28844032 | tf_op jit(solution)/shard_map/while/body/eval_jaxpr/hqk,khd->qhd/dot_general | solution.py:37
  737.8 13.8 %fusion.128 = (f32[4,512]{1,0:T(4,128)S(1)}, f32[4,512,3072]{2,1,0:T(8,128)}) fusion(bf16[512,4,128]{0,2,1:T(8,128)(2,1)} %bitcast.174, bf16[3072,4,128]{0,2,1:T(8,128)(2,1)S(1)} %bitcast.158), kind=kOutput, calls=%fused_computation.78.clone.1 | convolution fusion | flops 1629490176 | bytes 28844032 | tf_op jit(solution)/shard_map/while/body/eval_jaxpr/sub | solution.py:30
  753.7 11.3 %fusion.134 = f32[4,512,3072]{2,1,0:T(8,128)} fusion(bf16[512,4,128]{0,2,1:T(8,128)(2,1)} %bitcast.170, bf16[3072,4,128]{0,2,1:T(8,128)(2,1)S(1)} %bitcast.159), kind=kOutput, calls=%fused_computation.79.clone.1 | convolution fusion | flops 1610612736 | bytes 28835840 | tf_op jit(solution)/shard_map/while/body/eval_jaxpr/qhd,khd->hqk/dot_general | solution.py:26
  768.9 28.1 %multiply_reduce_fusion.7 = (f32[4,512]{1,0:T(4,128)S(1)}, f32[4,512,3072]{2,1,0:T(8,128)}) fusion(f32[4,512,3072]{2,1,0:T(8,128)} %get-tuple-element.400, f32[4,512]{1,0:T(4,128)S(1)} %get-tuple-element.401, f32[4,512,3072]{2,1,0:T(8,128)} %fusion.134, bf16[512,4,128]{0,2,1:T(8,128)(2,1)} %bitcast.175, bf16[3072,4,128]{0,2,1:T(8,128)(2,1)} %bitcast.166), kind=kOutput, calls=%fused_computation.6.clone.1 | convolution fusion | flops 1642067968 | bytes 79183872 | tf_op jit(solution)/shard_map/while/body/eval_jaxpr/qhd,khd->hqk/dot_general | solution.py:27
  799.0 12.7 %fusion.133 = f32[4,128,512]{2,1,0:T(8,128)} fusion(bf16[3072,4,128]{0,2,1:T(8,128)(2,1)S(1)} %bitcast.168, f32[4,512,3072]{2,1,0:T(8,128)} %get-tuple-element.400, f32[4,512]{1,0:T(4,128)S(1)} %get-tuple-element.401), kind=kOutput, calls=%fused_computation.26.clone.1 | convolution fusion | flops 1623195648 | bytes 29368320 | tf_op jit(solution)/shard_map/while/body/eval_jaxpr/hqk,khd->qhd/dot_general | solution.py:40
  812.9 18.7 %fusion.135 = bf16[4,128,512]{2,1,0:T(8,128)(2,1)} fusion(f32[4,128,512]{2,1,0:T(8,128)S(1)} %copy-done.15, bf16[3072,4,128]{0,2,1:T(8,128)(2,1)S(1)} %bitcast.162, f32[4,512,3072]{2,1,0:T(8,128)} %get-tuple-element.412, f32[4,512]{1,0:T(4,128)S(1)} %get-tuple-element.413, f32[4,512,3072]{2,1,0:T(8,128)} %get-tuple-element.400, ...), kind=kOutput, calls=%fused_computation.40.clone.1 | convolution fusion | flops 1636302848 | bytes 55066624 | tf_op jit(solution)/shard_map/while/body/eval_jaxpr/hqk,khd->qhd/dot_general | solution.py:38
  833.7 11.3 %fusion.131 = f32[4,512,3072]{2,1,0:T(8,128)} fusion(bf16[512,4,128]{0,2,1:T(8,128)(2,1)} %bitcast.171, bf16[3072,4,128]{0,2,1:T(8,128)(2,1)S(1)} %bitcast.160), kind=kOutput, calls=%fused_computation.80.clone.1 | convolution fusion | flops 1610612736 | bytes 28835840 | tf_op jit(solution)/shard_map/while/body/eval_jaxpr/qhd,khd->hqk/dot_general | solution.py:26
  847.0 13.7 %fusion.126 = (f32[4,512]{1,0:T(4,128)S(1)}, f32[4,512,3072]{2,1,0:T(8,128)}) fusion(bf16[512,4,128]{0,2,1:T(8,128)(2,1)} %bitcast.176, bf16[3072,4,128]{0,2,1:T(8,128)(2,1)S(1)} %bitcast.161), kind=kOutput, calls=%fused_computation.77.clone.1 | convolution fusion | flops 1629490176 | bytes 28844032 | tf_op jit(solution)/shard_map/while/body/eval_jaxpr/sub | solution.py:30
  860.8 28.2 %multiply_reduce_fusion.6 = (f32[4,512]{1,0:T(4,128)S(1)}, f32[4,512,3072]{2,1,0:T(8,128)}) fusion(f32[4,512,3072]{2,1,0:T(8,128)} %get-tuple-element.397, f32[4,512]{1,0:T(4,128)S(1)} %get-tuple-element.398, f32[4,512,3072]{2,1,0:T(8,128)} %fusion.131, bf16[512,4,128]{0,2,1:T(8,128)(2,1)} %bitcast.177, bf16[3072,4,128]{0,2,1:T(8,128)(2,1)} %bitcast.167), kind=kOutput, calls=%fused_computation.3.clone.1 | convolution fusion | flops 1642067968 | bytes 79183872 | tf_op jit(solution)/shard_map/while/body/eval_jaxpr/qhd,khd->hqk/dot_general | solution.py:27
  899.6 17.9 %fusion.132 = bf16[4,128,512]{2,1,0:T(8,128)(2,1)S(1)} fusion(f32[4,128,512]{2,1,0:T(8,128)S(1)} %fusion.130, bf16[3072,4,128]{0,2,1:T(8,128)(2,1)S(1)} %bitcast.164, f32[4,512,3072]{2,1,0:T(8,128)} %get-tuple-element.409, f32[4,512]{1,0:T(4,128)S(1)} %get-tuple-element.410, f32[4,512,3072]{2,1,0:T(8,128)} %get-tuple-element.397, ...), kind=kOutput, calls=%fused_computation.41.clone.1 | convolution fusion | flops 1636302848 | bytes 55066624 | tf_op jit(solution)/shard_map/while/body/eval_jaxpr/hqk,khd->qhd/dot_general | solution.py:38
  919.3 11.6 %fusion.129 = bf16[4,128,512]{2,1,0:T(8,128)(2,1)S(1)} fusion(bf16[3072,4,128]{0,2,1:T(8,128)(2,1)} %bitcast.163, f32[4,512,3072]{2,1,0:T(8,128)} %get-tuple-element.400, f32[4,512]{1,0:T(4,128)S(1)} %get-tuple-element.401), kind=kOutput, calls=%fused_computation.38.clone.1 | convolution fusion | flops 1623457792 | bytes 28844032 | tf_op jit(solution)/shard_map/while/body/eval_jaxpr/hqk,khd->qhd/dot_general | solution.py:37
  943.3 12.1 %convolution_bitcast_fusion = f32[3072,512]{0,1:T(8,128)} fusion(bf16[2048,512]{1,0:T(8,128)(2,1)} %bitcast.196, bf16[2048,3072]{1,0:T(8,128)(2,1)} %param.17), kind=kOutput, calls=%fused_computation.71 | convolution fusion | flops 6442450944 | bytes 20971520 | tf_op jit(solution)/shard_map/dot_general | solution.py:119
  957.0 53.7 %all_to_all.152 = bf16[8,256,512]{2,1,0:T(8,128)(2,1)} all-to-all(bf16[8,256,512]{2,1,0:T(8,128)(2,1)S(1)} %bitcast.197), channel_id=1, replica_groups=mesh['clip'=4,'head'=8] {'head'}, dimensions={0} | all-to-all | bytes 4194304 | tf_op jit(solution)/shard_map/all_to_all | solution.py:112
  1022.3 41.0 %all-to-all-done.7 = bf16[8,256,512]{2,1,0:T(8,128)(2,1)S(1)} async-done(((bf16[8,256,512]{2,1,0:T(8,128)(2,1)}), bf16[8,256,512]{2,1,0:T(8,128)(2,1)S(1)}, u32[]{:S(2)}, u32[]{:S(2)}) %all-to-all-start.7) | async-done | bytes 2097184 | tf_op jit(solution)/shard_map/all_to_all | solution.py:115
  (149 shorter events, 256.2 us)
Async XLA Ops:
  11.2 55.4 %all-to-all-start.2 = ((bf16[256,8,512]{0,2,1:T(8,128)(2,1)}), bf16[256,8,512]{0,2,1:T(8,128)(2,1)S(1)}, u32[]{:S(2)}, u32[]{:S(2)}) async-start(bf16[256,8,512]{0,2,1:T(8,128)(2,1)} %bitcast.189), calls=%async_computation.2 | async-start | bytes 4194304 | tf_op jit(solution)/shard_map/all_to_all | solution.py:50
  66.6 53.4 %all-to-all-start.4 = ((bf16[256,8,512]{0,2,1:T(8,128)(2,1)}), bf16[256,8,512]{0,2,1:T(8,128)(2,1)}, u32[]{:S(2)}, u32[]{:S(2)}) async-start(bf16[256,8,512]{0,2,1:T(8,128)(2,1)} %bitcast.184), calls=%async_computation.4 | async-start | bytes 4194304 | tf_op jit(solution)/shard_map/all_to_all | solution.py:53
  120.0 53.4 %all-to-all-start.5 = ((bf16[256,8,512]{0,2,1:T(8,128)(2,1)}), bf16[256,8,512]{0,2,1:T(8,128)(2,1)}, u32[]{:S(2)}, u32[]{:S(2)}) async-start(bf16[256,8,512]{0,2,1:T(8,128)(2,1)} %bitcast.185), calls=%async_computation.5 | async-start | bytes 4194304 | tf_op jit(solution)/shard_map/all_to_all | solution.py:54
  173.4 53.4 %all-to-all-start = ((bf16[256,8,512]{0,2,1:T(8,128)(2,1)}), bf16[256,8,512]{0,2,1:T(8,128)(2,1)}, u32[]{:S(2)}, u32[]{:S(2)}) async-start(bf16[256,8,512]{0,2,1:T(8,128)(2,1)} %bitcast.186), calls=%async_computation | async-start | bytes 4194304 | tf_op jit(solution)/shard_map/all_to_all | solution.py:51
  226.8 53.4 %all-to-all-start.1 = ((bf16[256,8,512]{0,2,1:T(8,128)(2,1)}), bf16[256,8,512]{0,2,1:T(8,128)(2,1)}, u32[]{:S(2)}, u32[]{:S(2)}) async-start(bf16[256,8,512]{0,2,1:T(8,128)(2,1)} %bitcast.187), calls=%async_computation.1 | async-start | bytes 4194304 | tf_op jit(solution)/shard_map/all_to_all | solution.py:49
  280.2 53.4 %all-to-all-start.3 = ((bf16[256,8,512]{0,2,1:T(8,128)(2,1)}), bf16[256,8,512]{0,2,1:T(8,128)(2,1)}, u32[]{:S(2)}, u32[]{:S(2)}) async-start(bf16[256,8,512]{0,2,1:T(8,128)(2,1)} %bitcast.182), calls=%async_computation.3 | async-start | bytes 4194304 | tf_op jit(solution)/shard_map/all_to_all | solution.py:52
  284.6 785.2 %reduce-scatter.2.cloned.1.call-start = ((), (), s32[]{:S(2)}) async-start(), calls=%async_computation.9 | async-start | bytes 7864320 | tf_op jit(solution)/shard_map/reduce_scatter | solution.py:122
  287.1 50.5 %collective-permute-start.1 = (bf16[2048,512]{1,0:T(8,128)(2,1)}, bf16[2048,512]{1,0:T(8,128)(2,1)}, u32[]{:S(2)}, u32[]{:S(2)}) collective-permute-start(bf16[2048,512]{1,0:T(8,128)(2,1)} %bitcast.194), channel_id=1, source_target_pairs={{0,8},{8,16},{16,24},{24,0},{1,9},{9,17},{17,25},{25,1},{2,10},{10... | collective-permute-start | bytes 6291464 | tf_op jit(solution)/shard_map/ppermute | solution.py:12
  292.5 89.2 %collective-permute-start.2 = (bf16[2048,512]{1,0:T(8,128)(2,1)}, bf16[2048,512]{1,0:T(8,128)(2,1)}, u32[]{:S(2)}, u32[]{:S(2)}) collective-permute-start(bf16[2048,512]{1,0:T(8,128)(2,1)} %bitcast.36), channel_id=1, source_target_pairs={{0,8},{8,16},{16,24},{24,0},{1,9},{9,17},{17,25},{25,1},{2,10},{10... | collective-permute-start | bytes 6291464 | tf_op jit(solution)/shard_map/ppermute | solution.py:12
  297.9 128.7 %collective-permute-start.3 = (bf16[2048,512]{1,0:T(8,128)(2,1)}, bf16[2048,512]{1,0:T(8,128)(2,1)}, u32[]{:S(2)}, u32[]{:S(2)}) collective-permute-start(bf16[2048,512]{1,0:T(8,128)(2,1)} %bitcast.39), channel_id=1, source_target_pairs={{0,8},{8,16},{16,24},{24,0},{1,9},{9,17},{17,25},{25,1},{2,10},{10... | collective-permute-start | bytes 6291464 | tf_op jit(solution)/shard_map/ppermute | solution.py:12
  302.3 168.7 %collective-permute-start = (bf16[2048,512]{1,0:T(8,128)(2,1)S(1)}, bf16[2048,512]{1,0:T(8,128)(2,1)}, u32[]{:S(2)}, u32[]{:S(2)}) collective-permute-start(bf16[2048,512]{1,0:T(8,128)(2,1)S(1)} %bitcast.192), channel_id=1, source_target_pairs={{0,8},{8,16},{16,24},{24,0},{1,9},{9,17},{17,25},{25,1},{2,10},{10... | collective-permute-start | bytes 6291464 | tf_op jit(solution)/shard_map/ppermute | solution.py:12
  533.0 11.3 %copy-start.3 = (bf16[4096,512]{0,1:T(8,128)(2,1)S(1)}, bf16[4096,512]{0,1:T(8,128)(2,1)}, u32[]{:S(2)}) copy-start(bf16[4096,512]{0,1:T(8,128)(2,1)} %get-tuple-element.466) | copy-start | bytes 12582916 | tf_op jit(solution)/shard_map/while
  533.0 11.3 %copy-start.4 = (bf16[4096,512]{0,1:T(8,128)(2,1)S(1)}, bf16[4096,512]{0,1:T(8,128)(2,1)}, u32[]{:S(2)}) copy-start(bf16[4096,512]{0,1:T(8,128)(2,1)} %get-tuple-element.467) | copy-start | bytes 12582916 | tf_op jit(solution)/shard_map/while
  578.3 12.7 %copy-start.8 = (bf16[3072,512]{0,1:T(8,128)(2,1)}, bf16[3072,512]{0,1:T(8,128)(2,1)S(1)}, u32[]{:S(2)}) copy-start(bf16[3072,512]{0,1:T(8,128)(2,1)S(1)} %pad_maximum_fusion.14) | copy-start | bytes 9437188 | tf_op jit(solution)/shard_map/while
  578.3 12.7 %copy-start = (bf16[1024,512]{0,1:T(8,128)(2,1)S(1)}, bf16[1024,512]{0,1:T(8,128)(2,1)}, u32[]{:S(2)}) copy-start(bf16[1024,512]{0,1:T(8,128)(2,1)} %get-tuple-element.391) | copy-start | bytes 3145732 | tf_op jit(solution)/shard_map/while
  578.3 12.7 %copy-start.1 = (bf16[1024,512]{0,1:T(8,128)(2,1)S(1)}, bf16[1024,512]{0,1:T(8,128)(2,1)}, u32[]{:S(2)}) copy-start(bf16[1024,512]{0,1:T(8,128)(2,1)} %get-tuple-element.390) | copy-start | bytes 3145732 | tf_op jit(solution)/shard_map/while
  578.3 12.7 %copy-start.2 = (bf16[1024,512]{0,1:T(8,128)(2,1)S(1)}, bf16[1024,512]{0,1:T(8,128)(2,1)}, u32[]{:S(2)}) copy-start(bf16[1024,512]{0,1:T(8,128)(2,1)} %get-tuple-element.392) | copy-start | bytes 3145732 | tf_op jit(solution)/shard_map/while
  591.3 19.7 %copy-start.5 = (bf16[3072,512]{0,1:T(8,128)(2,1)}, bf16[3072,512]{0,1:T(8,128)(2,1)S(1)}, u32[]{:S(2)}) copy-start(bf16[3072,512]{0,1:T(8,128)(2,1)S(1)} %pad_maximum_fusion.12) | copy-start | bytes 9437188 | tf_op jit(solution)/shard_map/while
  640.1 28.2 %copy-start.9 = (bf16[3072,512]{0,1:T(8,128)(2,1)S(1)}, bf16[3072,512]{0,1:T(8,128)(2,1)}, u32[]{:S(2)}) copy-start(bf16[3072,512]{0,1:T(8,128)(2,1)} %copy-done.8) | copy-start | bytes 9437188 | tf_op jit(solution)/shard_map/while
  678.9 17.9 %copy-start.10 = (bf16[4,128,512]{2,1,0:T(8,128)(2,1)S(1)}, bf16[4,128,512]{2,1,0:T(8,128)(2,1)}, u32[]{:S(2)}) copy-start(bf16[4,128,512]{2,1,0:T(8,128)(2,1)} %fusion.135) | copy-start | bytes 1572868 | tf_op jit(solution)/shard_map/while
  698.6 11.6 %copy-start.7 = (bf16[3072,512]{0,1:T(8,128)(2,1)S(1)}, bf16[3072,512]{0,1:T(8,128)(2,1)}, u32[]{:S(2)}) copy-start(bf16[3072,512]{0,1:T(8,128)(2,1)} %copy-done.5) | copy-start | bytes 9437188 | tf_op jit(solution)/shard_map/while
  753.7 11.3 %copy-start.3 = (bf16[4096,512]{0,1:T(8,128)(2,1)S(1)}, bf16[4096,512]{0,1:T(8,128)(2,1)}, u32[]{:S(2)}) copy-start(bf16[4096,512]{0,1:T(8,128)(2,1)} %get-tuple-element.466) | copy-start | bytes 12582916 | tf_op jit(solution)/shard_map/while
  753.7 11.3 %copy-start.4 = (bf16[4096,512]{0,1:T(8,128)(2,1)S(1)}, bf16[4096,512]{0,1:T(8,128)(2,1)}, u32[]{:S(2)}) copy-start(bf16[4096,512]{0,1:T(8,128)(2,1)} %get-tuple-element.467) | copy-start | bytes 12582916 | tf_op jit(solution)/shard_map/while
  799.0 12.7 %copy-start.8 = (bf16[3072,512]{0,1:T(8,128)(2,1)}, bf16[3072,512]{0,1:T(8,128)(2,1)S(1)}, u32[]{:S(2)}) copy-start(bf16[3072,512]{0,1:T(8,128)(2,1)S(1)} %pad_maximum_fusion.14) | copy-start | bytes 9437188 | tf_op jit(solution)/shard_map/while
  799.0 12.7 %copy-start = (bf16[1024,512]{0,1:T(8,128)(2,1)S(1)}, bf16[1024,512]{0,1:T(8,128)(2,1)}, u32[]{:S(2)}) copy-start(bf16[1024,512]{0,1:T(8,128)(2,1)} %get-tuple-element.391) | copy-start | bytes 3145732 | tf_op jit(solution)/shard_map/while
  799.0 12.7 %copy-start.1 = (bf16[1024,512]{0,1:T(8,128)(2,1)S(1)}, bf16[1024,512]{0,1:T(8,128)(2,1)}, u32[]{:S(2)}) copy-start(bf16[1024,512]{0,1:T(8,128)(2,1)} %get-tuple-element.390) | copy-start | bytes 3145732 | tf_op jit(solution)/shard_map/while
  799.0 12.7 %copy-start.2 = (bf16[1024,512]{0,1:T(8,128)(2,1)S(1)}, bf16[1024,512]{0,1:T(8,128)(2,1)}, u32[]{:S(2)}) copy-start(bf16[1024,512]{0,1:T(8,128)(2,1)} %get-tuple-element.392) | copy-start | bytes 3145732 | tf_op jit(solution)/shard_map/while
  812.0 19.7 %copy-start.5 = (bf16[3072,512]{0,1:T(8,128)(2,1)}, bf16[3072,512]{0,1:T(8,128)(2,1)S(1)}, u32[]{:S(2)}) copy-start(bf16[3072,512]{0,1:T(8,128)(2,1)S(1)} %pad_maximum_fusion.12) | copy-start | bytes 9437188 | tf_op jit(solution)/shard_map/while
  860.8 28.2 %copy-start.9 = (bf16[3072,512]{0,1:T(8,128)(2,1)S(1)}, bf16[3072,512]{0,1:T(8,128)(2,1)}, u32[]{:S(2)}) copy-start(bf16[3072,512]{0,1:T(8,128)(2,1)} %copy-done.8) | copy-start | bytes 9437188 | tf_op jit(solution)/shard_map/while
  899.6 17.9 %copy-start.10 = (bf16[4,128,512]{2,1,0:T(8,128)(2,1)S(1)}, bf16[4,128,512]{2,1,0:T(8,128)(2,1)}, u32[]{:S(2)}) copy-start(bf16[4,128,512]{2,1,0:T(8,128)(2,1)} %fusion.135) | copy-start | bytes 1572868 | tf_op jit(solution)/shard_map/while
  919.3 11.6 %copy-start.7 = (bf16[3072,512]{0,1:T(8,128)(2,1)S(1)}, bf16[3072,512]{0,1:T(8,128)(2,1)}, u32[]{:S(2)}) copy-start(bf16[3072,512]{0,1:T(8,128)(2,1)} %copy-done.5) | copy-start | bytes 9437188 | tf_op jit(solution)/shard_map/while
  1010.7 52.6 %all-to-all-start.7 = ((bf16[8,256,512]{2,1,0:T(8,128)(2,1)}), bf16[8,256,512]{2,1,0:T(8,128)(2,1)S(1)}, u32[]{:S(2)}, u32[]{:S(2)}) async-start(bf16[8,256,512]{2,1,0:T(8,128)(2,1)} %bitcast.198), calls=%async_computation.7 | async-start | bytes 4194304 | tf_op jit(solution)/shard_map/all_to_all | solution.py:115
  (10 other events, 58.3 us)
Sparse Core Ops, SparseCore 0:
  955.6 70.2 reduce-scatter.1
where the time goes:
time: 1090 us; the launch traced here: 1080 us
  waiting for transfers between devices  393 us (36%)
  matrix products  389 us (36%)
  local copies, waits for them, and re-layouts  140 us (13%)
  blocking collectives  53.7 us (5%)
  starting transfers between devices  36.8 us (3%)
  loops' own time  27 us (2%)
  other arithmetic  26 us (2%)
  between operations  14.5 us (1%)
    dot_general x4, matrix products, attend_block(): jnp.einsum('qhd,khd->hqk', query_block, ktan_win, preferred_element_type=...  113 us
    ppermute x4, waiting for transfers between devices, shifted(): lax.ppermute(shard, axis, [(i, (i + by) % length) for i in range(length)])  101 us
    dot_general x4, matrix products, attend_block(): jnp.einsum('hqk,khd->qhd', tangent_low, value_win, preferred_element_type...  73.2 us
    sub x4, matrix products, attend_block(): raw_weights = jnp.exp(scores - row_max)  55 us
    all_to_all x1, blocking collectives, on_device(): lax.all_to_all(as_sent(output_h), 'head', split_axis=0, concat_axis=1, ti...  53.7 us
    dot_general x4, matrix products, attend_block(): jnp.einsum('hqk,khd->qhd', prob_low, vtan_win, preferred_element_type=jnp...  46.6 us
    dot_general x4, matrix products, attend_block(): jnp.einsum('qhd,khd->hqk', qtan_block, key_win, preferred_element_type=jn...  45.2 us
    all_to_all x1, waiting for transfers between devices, on_device(): lax.all_to_all(key_rows, 'head', split_axis=1, concat_axis=0, tiled=True)  45 us
  transfers between devices with their start and end apart: 12, of which 10 were waited for; matrix products, arithmetic and copies ran while one was open for 8% of the time, Pallas kernels for 0%

commit v1 on v0

--- a/solution.py
+++ b/solution.py
@@ -5,6 +5,28 @@
 
 HDIM = 128
 CLIP = 1024
+
+
+def cut_along(x, dim, length):
+    before, after = (x.shape[:dim], x.shape[dim + 1 :])
+    return jnp.moveaxis(x.reshape(*before, length, -1, *after), dim, 0)
+
+
+def laid_out(pieces, dim):
+    pieces = jnp.moveaxis(pieces, 0, dim)
+    lengths = pieces.shape
+    return pieces.reshape(*lengths[:dim], lengths[dim] * lengths[dim + 1], *lengths[dim + 2 :])
+
+
+def sent_to_each(array, axis, split_dim, concat_dim):
+    count, here = (lax.axis_size(axis), lax.axis_index(axis))
+    blocks = cut_along(array, split_dim, count)
+    outs = [blocks[here]]
+    for step in range(1, count):
+        sent = blocks[(here + step) % count]
+        outs.append(lax.ppermute(sent, axis, [(i, (i + step) % count) for i in range(count)]))
+    blocks = jnp.stack(outs)[(here - jnp.arange(count)) % count]
+    return laid_out(blocks, concat_dim)
 
 
 def shifted(shard, axis, by):
@@ -109,9 +131,7 @@
     output_h = results[0].reshape(group_rows, cols_here)
     tangent_h = results[1].reshape(group_rows, cols_here)
     attended, attended_tangent = (
-        lax.all_to_all(as_sent(output_h), "head", split_axis=0, concat_axis=1, tiled=True).astype(
-            output_h.dtype
-        ),
+        sent_to_each(as_sent(output_h), "head", 0, 1).astype(output_h.dtype),
         lax.all_to_all(as_sent(tangent_h), "head", split_axis=0, concat_axis=1, tiled=True).astype(
             tangent_h.dtype
         ),

time: 1090 us -> 1090 us (level)
  blocking collectives: 53.7 us -> 0 us
  waiting for transfers between devices: 393 us -> 415 us
  starting transfers between devices: 36.8 us -> 48.6 us
    ppermute x0 -> x7, waiting for transfers between devices: none -> 62.7 us  [sent_to_each(): lax.ppermute(sent, axis, [(i, (i + step) % count) for i in range(count)])]
    all_to_all x1 -> x0, blocking collectives: 53.7 us -> none  [on_device(): lax.all_to_all(as_sent(output_h), 'head', split_axis=0, concat_axis=1, ti...]
    all_to_all x1, waiting for transfers between devices: 41 us -> 0.01 us  [on_device(): lax.all_to_all(as_sent(tangent_h), 'head', split_axis=0, concat_axis=1, t...]
    unnamed x13 -> x17, local copies, waits for them, and re-layouts: 37.2 us -> 40 us
  transfers between devices with their start and end apart: 12 -> 19, of which waited for: 10 -> 13; matrix products, arithmetic and copies ran while one was open for 8% -> 9% of each run, Pallas kernels for 0% -> 0%
where the time goes in v1:
time: 1090 us; the launch traced here: 1070 us
  waiting for transfers between devices  415 us (38%)
  matrix products  390 us (36%)
  local copies, waits for them, and re-layouts  149 us (14%)
  starting transfers between devices  48.6 us (4%)
  loops' own time  26.9 us (2%)
  other arithmetic  26.1 us (2%)
  between operations  14.5 us (1%)
    dot_general x4, matrix products, attend_block(): jnp.einsum('qhd,khd->hqk', query_block, ktan_win, preferred_element_type=...  113 us
    ppermute x4, waiting for transfers between devices, shifted(): lax.ppermute(shard, axis, [(i, (i + by) % length) for i in range(length)])  101 us
    dot_general x4, matrix products, attend_block(): jnp.einsum('hqk,khd->qhd', tangent_low, value_win, preferred_element_type...  73.2 us
    ppermute x7, waiting for transfers between devices, sent_to_each(): lax.ppermute(sent, axis, [(i, (i + step) % count) for i in range(count)])  62.7 us
    sub x4, matrix products, attend_block(): raw_weights = jnp.exp(scores - row_max)  55 us
    dot_general x4, matrix products, attend_block(): jnp.einsum('hqk,khd->qhd', prob_low, vtan_win, preferred_element_type=jnp...  46.6 us
    dot_general x4, matrix products, attend_block(): jnp.einsum('qhd,khd->hqk', qtan_block, key_win, preferred_element_type=jn...  45.4 us
    all_to_all x1, waiting for transfers between devices, on_device(): lax.all_to_all(key_rows, 'head', split_axis=1, concat_axis=0, tiled=True)  45 us
  transfers between devices with their start and end apart: 19, of which 13 were waited for; matrix products, arithmetic and copies ran while one was open for 9% of the time, Pallas kernels for 0%

profile of v1, /device:TPU:0, one launch (start us, length us, event | category | flops | bytes accessed | tf_op | source)
XLA Modules:
  0.0 1069.7 jit_solution(5242028195973816457)
XLA Ops:
  21.7 45.0 %all-to-all-done.2 = bf16[256,8,512]{0,2,1:T(8,128)(2,1)S(1)} async-done(((bf16[256,8,512]{0,2,1:T(8,128)(2,1)}), bf16[256,8,512]{0,2,1:T(8,128)(2,1)S(1)}, u32[]{:S(2)}, u32[]{:S(2)}) %all-to-all-start.2) | async-done | bytes 2097184 | tf_op jit(solution)/shard_map/all_to_all | solution.py:72
  75.1 44.9 %all-to-all-done.4 = bf16[256,8,512]{0,2,1:T(8,128)(2,1)} async-done(((bf16[256,8,512]{0,2,1:T(8,128)(2,1)}), bf16[256,8,512]{0,2,1:T(8,128)(2,1)}, u32[]{:S(2)}, u32[]{:S(2)}) %all-to-all-start.4) | async-done | bytes 2097184 | tf_op jit(solution)/shard_map/all_to_all | solution.py:75
  128.5 45.0 %all-to-all-done.5 = bf16[256,8,512]{0,2,1:T(8,128)(2,1)} async-done(((bf16[256,8,512]{0,2,1:T(8,128)(2,1)}), bf16[256,8,512]{0,2,1:T(8,128)(2,1)}, u32[]{:S(2)}, u32[]{:S(2)}) %all-to-all-start.5) | async-done | bytes 2097184 | tf_op jit(solution)/shard_map/all_to_all | solution.py:76
  181.9 45.0 %all-to-all-done = bf16[256,8,512]{0,2,1:T(8,128)(2,1)} async-done(((bf16[256,8,512]{0,2,1:T(8,128)(2,1)}), bf16[256,8,512]{0,2,1:T(8,128)(2,1)}, u32[]{:S(2)}, u32[]{:S(2)}) %all-to-all-start) | async-done | bytes 2097184 | tf_op jit(solution)/shard_map/all_to_all | solution.py:73
  235.3 44.9 %all-to-all-done.1 = bf16[256,8,512]{0,2,1:T(8,128)(2,1)} async-done(((bf16[256,8,512]{0,2,1:T(8,128)(2,1)}), bf16[256,8,512]{0,2,1:T(8,128)(2,1)}, u32[]{:S(2)}, u32[]{:S(2)}) %all-to-all-start.1) | async-done | bytes 2097184 | tf_op jit(solution)/shard_map/all_to_all | solution.py:71
  306.9 26.8 %all-to-all-done.3 = bf16[256,8,512]{0,2,1:T(8,128)(2,1)} async-done(((bf16[256,8,512]{0,2,1:T(8,128)(2,1)}), bf16[256,8,512]{0,2,1:T(8,128)(2,1)}, u32[]{:S(2)}, u32[]{:S(2)}) %all-to-all-start.3) | async-done | bytes 2097184 | tf_op jit(solution)/shard_map/all_to_all | solution.py:74
  348.4 33.3 %collective-permute-done.2 = bf16[2048,512]{1,0:T(8,128)(2,1)} collective-permute-done((bf16[2048,512]{1,0:T(8,128)(2,1)}, bf16[2048,512]{1,0:T(8,128)(2,1)}, u32[]{:S(2)}, u32[]{:S(2)}) %collective-permute-start.2) | collective-permute-done | bytes 2097184 | tf_op jit(solution)/shard_map/ppermute | solution.py:34
  392.6 34.1 %collective-permute-done.3 = bf16[2048,512]{1,0:T(8,128)(2,1)} collective-permute-done((bf16[2048,512]{1,0:T(8,128)(2,1)}, bf16[2048,512]{1,0:T(8,128)(2,1)}, u32[]{:S(2)}, u32[]{:S(2)}) %collective-permute-start.3) | collective-permute-done | bytes 2097184 | tf_op jit(solution)/shard_map/ppermute | solution.py:34
  437.6 33.4 %collective-permute-done = bf16[2048,512]{1,0:T(8,128)(2,1)} collective-permute-done((bf16[2048,512]{1,0:T(8,128)(2,1)S(1)}, bf16[2048,512]{1,0:T(8,128)(2,1)}, u32[]{:S(2)}, u32[]{:S(2)}) %collective-permute-start) | collective-permute-done | bytes 2097184 | tf_op jit(solution)/shard_map/ppermute | solution.py:34
  481.8 462.0 %while.14 = (s32[]{:T(128)}, bf16[2,1024,512]{2,1,0:T(8,128)(2,1)}, bf16[2,1024,512]{2,1,0:T(8,128)(2,1)}, s32[2]{0:T(128)}, bf16[4096,512]{0,1:T(8,128)(2,1)}, ...) while((s32[]{:T(128)}, bf16[2,1024,512]{2,1,0:T(8,128)(2,1)}, ...), condition=%wide.region_7.8_spmd, body=%wide.region_0.7_spmd.sunk | while | flops 19572197376 | bytes 686934336 | solution.py:130
  517.0 13.8 %fusion.130 = (f32[4,512]{1,0:T(4,128)S(1)}, f32[4,512,3072]{2,1,0:T(8,128)}) fusion(bf16[512,4,128]{0,2,1:T(8,128)(2,1)} %bitcast.204, bf16[3072,4,128]{0,2,1:T(8,128)(2,1)S(1)} %bitcast.188), kind=kOutput, calls=%fused_computation.101.clone.1 | convolution fusion | flops 1629490176 | bytes 28844032 | tf_op jit(solution)/shard_map/while/body/eval_jaxpr/sub | solution.py:52
  532.9 11.4 %fusion.136 = f32[4,512,3072]{2,1,0:T(8,128)} fusion(bf16[512,4,128]{0,2,1:T(8,128)(2,1)} %bitcast.200, bf16[3072,4,128]{0,2,1:T(8,128)(2,1)S(1)} %bitcast.189), kind=kOutput, calls=%fused_computation.102.clone.1 | convolution fusion | flops 1610612736 | bytes 28835840 | tf_op jit(solution)/shard_map/while/body/eval_jaxpr/qhd,khd->hqk/dot_general | solution.py:48
  548.2 28.2 %multiply_reduce_fusion.7 = (f32[4,512]{1,0:T(4,128)S(1)}, f32[4,512,3072]{2,1,0:T(8,128)}) fusion(f32[4,512,3072]{2,1,0:T(8,128)} %get-tuple-element.408, f32[4,512]{1,0:T(4,128)S(1)} %get-tuple-element.409, f32[4,512,3072]{2,1,0:T(8,128)} %fusion.136, bf16[512,4,128]{0,2,1:T(8,128)(2,1)} %bitcast.205, bf16[3072,4,128]{0,2,1:T(8,128)(2,1)} %bitcast.196), kind=kOutput, calls=%fused_computation.7.clone.1 | convolution fusion | flops 1642067968 | bytes 79183872 | tf_op jit(solution)/shard_map/while/body/eval_jaxpr/qhd,khd->hqk/dot_general | solution.py:49
  578.4 12.7 %fusion.135 = f32[4,128,512]{2,1,0:T(8,128)} fusion(bf16[3072,4,128]{0,2,1:T(8,128)(2,1)S(1)} %bitcast.198, f32[4,512,3072]{2,1,0:T(8,128)} %get-tuple-element.408, f32[4,512]{1,0:T(4,128)S(1)} %get-tuple-element.409), kind=kOutput, calls=%fused_computation.27.clone.1 | convolution fusion | flops 1623195648 | bytes 29368320 | tf_op jit(solution)/shard_map/while/body/eval_jaxpr/hqk,khd->qhd/dot_general | solution.py:62
  592.4 18.7 %fusion.137 = bf16[4,128,512]{2,1,0:T(8,128)(2,1)} fusion(f32[4,128,512]{2,1,0:T(8,128)S(1)} %copy-done.14, bf16[3072,4,128]{0,2,1:T(8,128)(2,1)S(1)} %bitcast.192, f32[4,512,3072]{2,1,0:T(8,128)} %get-tuple-element.420, f32[4,512]{1,0:T(4,128)S(1)} %get-tuple-element.421, f32[4,512,3072]{2,1,0:T(8,128)} %get-tuple-element.408, ...), kind=kOutput, calls=%fused_computation.41.clone.1 | convolution fusion | flops 1636302848 | bytes 55066624 | tf_op jit(solution)/shard_map/while/body/eval_jaxpr/hqk,khd->qhd/dot_general | solution.py:60
  613.1 11.3 %fusion.133 = f32[4,512,3072]{2,1,0:T(8,128)} fusion(bf16[512,4,128]{0,2,1:T(8,128)(2,1)} %bitcast.201, bf16[3072,4,128]{0,2,1:T(8,128)(2,1)S(1)} %bitcast.190), kind=kOutput, calls=%fused_computation.103.clone.1 | convolution fusion | flops 1610612736 | bytes 28835840 | tf_op jit(solution)/shard_map/while/body/eval_jaxpr/qhd,khd->hqk/dot_general | solution.py:48
  626.4 13.7 %fusion.128 = (f32[4,512]{1,0:T(4,128)S(1)}, f32[4,512,3072]{2,1,0:T(8,128)}) fusion(bf16[512,4,128]{0,2,1:T(8,128)(2,1)} %bitcast.206, bf16[3072,4,128]{0,2,1:T(8,128)(2,1)S(1)} %bitcast.191), kind=kOutput, calls=%fused_computation.100.clone.1 | convolution fusion | flops 1629490176 | bytes 28844032 | tf_op jit(solution)/shard_map/while/body/eval_jaxpr/sub | solution.py:52
  640.1 28.4 %multiply_reduce_fusion.6 = (f32[4,512]{1,0:T(4,128)S(1)}, f32[4,512,3072]{2,1,0:T(8,128)}) fusion(f32[4,512,3072]{2,1,0:T(8,128)} %get-tuple-element.405, f32[4,512]{1,0:T(4,128)S(1)} %get-tuple-element.406, f32[4,512,3072]{2,1,0:T(8,128)} %fusion.133, bf16[512,4,128]{0,2,1:T(8,128)(2,1)} %bitcast.207, bf16[3072,4,128]{0,2,1:T(8,128)(2,1)} %bitcast.197), kind=kOutput, calls=%fused_computation.4.clone.1 | convolution fusion | flops 1642067968 | bytes 79183872 | tf_op jit(solution)/shard_map/while/body/eval_jaxpr/qhd,khd->hqk/dot_general | solution.py:49
  679.2 17.9 %fusion.134 = bf16[4,128,512]{2,1,0:T(8,128)(2,1)S(1)} fusion(f32[4,128,512]{2,1,0:T(8,128)S(1)} %fusion.132, bf16[3072,4,128]{0,2,1:T(8,128)(2,1)S(1)} %bitcast.194, f32[4,512,3072]{2,1,0:T(8,128)} %get-tuple-element.417, f32[4,512]{1,0:T(4,128)S(1)} %get-tuple-element.418, f32[4,512,3072]{2,1,0:T(8,128)} %get-tuple-element.405, ...), kind=kOutput, calls=%fused_computation.42.clone.1 | convolution fusion | flops 1636302848 | bytes 55066624 | tf_op jit(solution)/shard_map/while/body/eval_jaxpr/hqk,khd->qhd/dot_general | solution.py:60
  698.8 11.6 %fusion.131 = bf16[4,128,512]{2,1,0:T(8,128)(2,1)S(1)} fusion(bf16[3072,4,128]{0,2,1:T(8,128)(2,1)} %bitcast.193, f32[4,512,3072]{2,1,0:T(8,128)} %get-tuple-element.408, f32[4,512]{1,0:T(4,128)S(1)} %get-tuple-element.409), kind=kOutput, calls=%fused_computation.39.clone.1 | convolution fusion | flops 1623457792 | bytes 28844032 | tf_op jit(solution)/shard_map/while/body/eval_jaxpr/hqk,khd->qhd/dot_general | solution.py:59
  737.9 13.8 %fusion.130 = (f32[4,512]{1,0:T(4,128)S(1)}, f32[4,512,3072]{2,1,0:T(8,128)}) fusion(bf16[512,4,128]{0,2,1:T(8,128)(2,1)} %bitcast.204, bf16[3072,4,128]{0,2,1:T(8,128)(2,1)S(1)} %bitcast.188), kind=kOutput, calls=%fused_computation.101.clone.1 | convolution fusion | flops 1629490176 | bytes 28844032 | tf_op jit(solution)/shard_map/while/body/eval_jaxpr/sub | solution.py:52
  753.8 11.4 %fusion.136 = f32[4,512,3072]{2,1,0:T(8,128)} fusion(bf16[512,4,128]{0,2,1:T(8,128)(2,1)} %bitcast.200, bf16[3072,4,128]{0,2,1:T(8,128)(2,1)S(1)} %bitcast.189), kind=kOutput, calls=%fused_computation.102.clone.1 | convolution fusion | flops 1610612736 | bytes 28835840 | tf_op jit(solution)/shard_map/while/body/eval_jaxpr/qhd,khd->hqk/dot_general | solution.py:48
  769.1 28.2 %multiply_reduce_fusion.7 = (f32[4,512]{1,0:T(4,128)S(1)}, f32[4,512,3072]{2,1,0:T(8,128)}) fusion(f32[4,512,3072]{2,1,0:T(8,128)} %get-tuple-element.408, f32[4,512]{1,0:T(4,128)S(1)} %get-tuple-element.409, f32[4,512,3072]{2,1,0:T(8,128)} %fusion.136, bf16[512,4,128]{0,2,1:T(8,128)(2,1)} %bitcast.205, bf16[3072,4,128]{0,2,1:T(8,128)(2,1)} %bitcast.196), kind=kOutput, calls=%fused_computation.7.clone.1 | convolution fusion | flops 1642067968 | bytes 79183872 | tf_op jit(solution)/shard_map/while/body/eval_jaxpr/qhd,khd->hqk/dot_general | solution.py:49
  799.3 12.7 %fusion.135 = f32[4,128,512]{2,1,0:T(8,128)} fusion(bf16[3072,4,128]{0,2,1:T(8,128)(2,1)S(1)} %bitcast.198, f32[4,512,3072]{2,1,0:T(8,128)} %get-tuple-element.408, f32[4,512]{1,0:T(4,128)S(1)} %get-tuple-element.409), kind=kOutput, calls=%fused_computation.27.clone.1 | convolution fusion | flops 1623195648 | bytes 29368320 | tf_op jit(solution)/shard_map/while/body/eval_jaxpr/hqk,khd->qhd/dot_general | solution.py:62
  813.3 18.7 %fusion.137 = bf16[4,128,512]{2,1,0:T(8,128)(2,1)} fusion(f32[4,128,512]{2,1,0:T(8,128)S(1)} %copy-done.14, bf16[3072,4,128]{0,2,1:T(8,128)(2,1)S(1)} %bitcast.192, f32[4,512,3072]{2,1,0:T(8,128)} %get-tuple-element.420, f32[4,512]{1,0:T(4,128)S(1)} %get-tuple-element.421, f32[4,512,3072]{2,1,0:T(8,128)} %get-tuple-element.408, ...), kind=kOutput, calls=%fused_computation.41.clone.1 | convolution fusion | flops 1636302848 | bytes 55066624 | tf_op jit(solution)/shard_map/while/body/eval_jaxpr/hqk,khd->qhd/dot_general | solution.py:60
  847.4 13.7 %fusion.128 = (f32[4,512]{1,0:T(4,128)S(1)}, f32[4,512,3072]{2,1,0:T(8,128)}) fusion(bf16[512,4,128]{0,2,1:T(8,128)(2,1)} %bitcast.206, bf16[3072,4,128]{0,2,1:T(8,128)(2,1)S(1)} %bitcast.191), kind=kOutput, calls=%fused_computation.100.clone.1 | convolution fusion | flops 1629490176 | bytes 28844032 | tf_op jit(solution)/shard_map/while/body/eval_jaxpr/sub | solution.py:52
  861.1 28.4 %multiply_reduce_fusion.6 = (f32[4,512]{1,0:T(4,128)S(1)}, f32[4,512,3072]{2,1,0:T(8,128)}) fusion(f32[4,512,3072]{2,1,0:T(8,128)} %get-tuple-element.405, f32[4,512]{1,0:T(4,128)S(1)} %get-tuple-element.406, f32[4,512,3072]{2,1,0:T(8,128)} %fusion.133, bf16[512,4,128]{0,2,1:T(8,128)(2,1)} %bitcast.207, bf16[3072,4,128]{0,2,1:T(8,128)(2,1)} %bitcast.197), kind=kOutput, calls=%fused_computation.4.clone.1 | convolution fusion | flops 1642067968 | bytes 79183872 | tf_op jit(solution)/shard_map/while/body/eval_jaxpr/qhd,khd->hqk/dot_general | solution.py:49
  900.1 17.9 %fusion.134 = bf16[4,128,512]{2,1,0:T(8,128)(2,1)S(1)} fusion(f32[4,128,512]{2,1,0:T(8,128)S(1)} %fusion.132, bf16[3072,4,128]{0,2,1:T(8,128)(2,1)S(1)} %bitcast.194, f32[4,512,3072]{2,1,0:T(8,128)} %get-tuple-element.417, f32[4,512]{1,0:T(4,128)S(1)} %get-tuple-element.418, f32[4,512,3072]{2,1,0:T(8,128)} %get-tuple-element.405, ...), kind=kOutput, calls=%fused_computation.42.clone.1 | convolution fusion | flops 1636302848 | bytes 55066624 | tf_op jit(solution)/shard_map/while/body/eval_jaxpr/hqk,khd->qhd/dot_general | solution.py:60
  919.7 11.6 %fusion.131 = bf16[4,128,512]{2,1,0:T(8,128)(2,1)S(1)} fusion(bf16[3072,4,128]{0,2,1:T(8,128)(2,1)} %bitcast.193, f32[4,512,3072]{2,1,0:T(8,128)} %get-tuple-element.408, f32[4,512]{1,0:T(4,128)S(1)} %get-tuple-element.409), kind=kOutput, calls=%fused_computation.39.clone.1 | convolution fusion | flops 1623457792 | bytes 28844032 | tf_op jit(solution)/shard_map/while/body/eval_jaxpr/hqk,khd->qhd/dot_general | solution.py:59
  943.8 12.0 %convolution_bitcast_fusion = f32[3072,512]{0,1:T(8,128)} fusion(bf16[2048,512]{1,0:T(8,128)(2,1)} %bitcast.226, bf16[2048,3072]{1,0:T(8,128)(2,1)} %param.17), kind=kOutput, calls=%fused_computation.72 | convolution fusion | flops 6442450944 | bytes 20971520 | tf_op jit(solution)/shard_map/dot_general | solution.py:139
  969.9 34.6 %collective-permute-done.4 = bf16[256,512]{1,0:T(8,128)(2,1)S(1)} collective-permute-done((bf16[256,512]{1,0:T(8,128)(2,1)S(1)}, bf16[256,512]{1,0:T(8,128)(2,1)S(1)}, u32[]{:S(2)}, u32[]{:S(2)}) %collective-permute-start.4) | collective-permute-done | bytes 262176 | tf_op jit(solution)/shard_map/ppermute | solution.py:27
  1010.0 27.2 %collective-permute-done.6 = bf16[256,512]{1,0:T(8,128)(2,1)S(1)} collective-permute-done((bf16[256,512]{1,0:T(8,128)(2,1)S(1)}, bf16[256,512]{1,0:T(8,128)(2,1)S(1)}, u32[]{:S(2)}, u32[]{:S(2)}) %collective-permute-start.6) | collective-permute-done | bytes 262176 | tf_op jit(solution)/shard_map/ppermute | solution.py:27
  (171 shorter events, 278.3 us)
Async XLA Ops:
  11.2 55.4 %all-to-all-start.2 = ((bf16[256,8,512]{0,2,1:T(8,128)(2,1)}), bf16[256,8,512]{0,2,1:T(8,128)(2,1)S(1)}, u32[]{:S(2)}, u32[]{:S(2)}) async-start(bf16[256,8,512]{0,2,1:T(8,128)(2,1)} %bitcast.218), calls=%async_computation.2 | async-start | bytes 4194304 | tf_op jit(solution)/shard_map/all_to_all | solution.py:72
  66.6 53.4 %all-to-all-start.4 = ((bf16[256,8,512]{0,2,1:T(8,128)(2,1)}), bf16[256,8,512]{0,2,1:T(8,128)(2,1)}, u32[]{:S(2)}, u32[]{:S(2)}) async-start(bf16[256,8,512]{0,2,1:T(8,128)(2,1)} %bitcast.214), calls=%async_computation.4 | async-start | bytes 4194304 | tf_op jit(solution)/shard_map/all_to_all | solution.py:75
  120.0 53.4 %all-to-all-start.5 = ((bf16[256,8,512]{0,2,1:T(8,128)(2,1)}), bf16[256,8,512]{0,2,1:T(8,128)(2,1)}, u32[]{:S(2)}, u32[]{:S(2)}) async-start(bf16[256,8,512]{0,2,1:T(8,128)(2,1)} %bitcast.215), calls=%async_computation.5 | async-start | bytes 4194304 | tf_op jit(solution)/shard_map/all_to_all | solution.py:76
  173.5 53.4 %all-to-all-start = ((bf16[256,8,512]{0,2,1:T(8,128)(2,1)}), bf16[256,8,512]{0,2,1:T(8,128)(2,1)}, u32[]{:S(2)}, u32[]{:S(2)}) async-start(bf16[256,8,512]{0,2,1:T(8,128)(2,1)} %bitcast.216), calls=%async_computation | async-start | bytes 4194304 | tf_op jit(solution)/shard_map/all_to_all | solution.py:73
  226.8 53.4 %all-to-all-start.1 = ((bf16[256,8,512]{0,2,1:T(8,128)(2,1)}), bf16[256,8,512]{0,2,1:T(8,128)(2,1)}, u32[]{:S(2)}, u32[]{:S(2)}) async-start(bf16[256,8,512]{0,2,1:T(8,128)(2,1)} %bitcast.217), calls=%async_computation.1 | async-start | bytes 4194304 | tf_op jit(solution)/shard_map/all_to_all | solution.py:71
  280.3 53.4 %all-to-all-start.3 = ((bf16[256,8,512]{0,2,1:T(8,128)(2,1)}), bf16[256,8,512]{0,2,1:T(8,128)(2,1)}, u32[]{:S(2)}, u32[]{:S(2)}) async-start(bf16[256,8,512]{0,2,1:T(8,128)(2,1)} %bitcast.213), calls=%async_computation.3 | async-start | bytes 4194304 | tf_op jit(solution)/shard_map/all_to_all | solution.py:74
  284.6 774.8 %reduce-scatter.2.cloned.1.call-start = ((), (), s32[]{:S(2)}) async-start(), calls=%async_computation.8 | async-start | bytes 7864320 | tf_op jit(solution)/shard_map/reduce_scatter | solution.py:142
  287.1 50.5 %collective-permute-start.1 = (bf16[2048,512]{1,0:T(8,128)(2,1)}, bf16[2048,512]{1,0:T(8,128)(2,1)}, u32[]{:S(2)}, u32[]{:S(2)}) collective-permute-start(bf16[2048,512]{1,0:T(8,128)(2,1)} %bitcast.224), channel_id=1, source_target_pairs={{0,8},{8,16},{16,24},{24,0},{1,9},{9,17},{17,25},{25,1},{2,10},{10... | collective-permute-start | bytes 6291464 | tf_op jit(solution)/shard_map/ppermute | solution.py:34
  292.6 89.2 %collective-permute-start.2 = (bf16[2048,512]{1,0:T(8,128)(2,1)}, bf16[2048,512]{1,0:T(8,128)(2,1)}, u32[]{:S(2)}, u32[]{:S(2)}) collective-permute-start(bf16[2048,512]{1,0:T(8,128)(2,1)} %bitcast.36), channel_id=1, source_target_pairs={{0,8},{8,16},{16,24},{24,0},{1,9},{9,17},{17,25},{25,1},{2,10},{10... | collective-permute-start | bytes 6291464 | tf_op jit(solution)/shard_map/ppermute | solution.py:34
  298.0 128.7 %collective-permute-start.3 = (bf16[2048,512]{1,0:T(8,128)(2,1)}, bf16[2048,512]{1,0:T(8,128)(2,1)}, u32[]{:S(2)}, u32[]{:S(2)}) collective-permute-start(bf16[2048,512]{1,0:T(8,128)(2,1)} %bitcast.39), channel_id=1, source_target_pairs={{0,8},{8,16},{16,24},{24,0},{1,9},{9,17},{17,25},{25,1},{2,10},{10... | collective-permute-start | bytes 6291464 | tf_op jit(solution)/shard_map/ppermute | solution.py:34
  302.3 168.7 %collective-permute-start = (bf16[2048,512]{1,0:T(8,128)(2,1)S(1)}, bf16[2048,512]{1,0:T(8,128)(2,1)}, u32[]{:S(2)}, u32[]{:S(2)}) collective-permute-start(bf16[2048,512]{1,0:T(8,128)(2,1)S(1)} %bitcast.222), channel_id=1, source_target_pairs={{0,8},{8,16},{16,24},{24,0},{1,9},{9,17},{17,25},{25,1},{2,10},{10... | collective-permute-start | bytes 6291464 | tf_op jit(solution)/shard_map/ppermute | solution.py:34
  578.3 12.7 %copy-start.8 = (bf16[3072,512]{0,1:T(8,128)(2,1)}, bf16[3072,512]{0,1:T(8,128)(2,1)S(1)}, u32[]{:S(2)}) copy-start(bf16[3072,512]{0,1:T(8,128)(2,1)S(1)} %pad_maximum_fusion.14) | copy-start | bytes 9437188 | tf_op jit(solution)/shard_map/while
  578.4 12.7 %copy-start = (bf16[1024,512]{0,1:T(8,128)(2,1)S(1)}, bf16[1024,512]{0,1:T(8,128)(2,1)}, u32[]{:S(2)}) copy-start(bf16[1024,512]{0,1:T(8,128)(2,1)} %get-tuple-element.399) | copy-start | bytes 3145732 | tf_op jit(solution)/shard_map/while
  578.4 12.7 %copy-start.1 = (bf16[1024,512]{0,1:T(8,128)(2,1)S(1)}, bf16[1024,512]{0,1:T(8,128)(2,1)}, u32[]{:S(2)}) copy-start(bf16[1024,512]{0,1:T(8,128)(2,1)} %get-tuple-element.398) | copy-start | bytes 3145732 | tf_op jit(solution)/shard_map/while
  578.4 12.7 %copy-start.2 = (bf16[1024,512]{0,1:T(8,128)(2,1)S(1)}, bf16[1024,512]{0,1:T(8,128)(2,1)}, u32[]{:S(2)}) copy-start(bf16[1024,512]{0,1:T(8,128)(2,1)} %get-tuple-element.400) | copy-start | bytes 3145732 | tf_op jit(solution)/shard_map/while
  591.4 19.7 %copy-start.5 = (bf16[3072,512]{0,1:T(8,128)(2,1)}, bf16[3072,512]{0,1:T(8,128)(2,1)S(1)}, u32[]{:S(2)}) copy-start(bf16[3072,512]{0,1:T(8,128)(2,1)S(1)} %pad_maximum_fusion.12) | copy-start | bytes 9437188 | tf_op jit(solution)/shard_map/while
  640.1 28.4 %copy-start.9 = (bf16[3072,512]{0,1:T(8,128)(2,1)S(1)}, bf16[3072,512]{0,1:T(8,128)(2,1)}, u32[]{:S(2)}) copy-start(bf16[3072,512]{0,1:T(8,128)(2,1)} %copy-done.8) | copy-start | bytes 9437188 | tf_op jit(solution)/shard_map/while
  679.2 17.9 %copy-start.10 = (bf16[4,128,512]{2,1,0:T(8,128)(2,1)S(1)}, bf16[4,128,512]{2,1,0:T(8,128)(2,1)}, u32[]{:S(2)}) copy-start(bf16[4,128,512]{2,1,0:T(8,128)(2,1)} %fusion.137) | copy-start | bytes 1572868 | tf_op jit(solution)/shard_map/while
  799.3 12.7 %copy-start.8 = (bf16[3072,512]{0,1:T(8,128)(2,1)}, bf16[3072,512]{0,1:T(8,128)(2,1)S(1)}, u32[]{:S(2)}) copy-start(bf16[3072,512]{0,1:T(8,128)(2,1)S(1)} %pad_maximum_fusion.14) | copy-start | bytes 9437188 | tf_op jit(solution)/shard_map/while
  799.3 12.7 %copy-start = (bf16[1024,512]{0,1:T(8,128)(2,1)S(1)}, bf16[1024,512]{0,1:T(8,128)(2,1)}, u32[]{:S(2)}) copy-start(bf16[1024,512]{0,1:T(8,128)(2,1)} %get-tuple-element.399) | copy-start | bytes 3145732 | tf_op jit(solution)/shard_map/while
  799.3 12.7 %copy-start.1 = (bf16[1024,512]{0,1:T(8,128)(2,1)S(1)}, bf16[1024,512]{0,1:T(8,128)(2,1)}, u32[]{:S(2)}) copy-start(bf16[1024,512]{0,1:T(8,128)(2,1)} %get-tuple-element.398) | copy-start | bytes 3145732 | tf_op jit(solution)/shard_map/while
  812.3 19.7 %copy-start.5 = (bf16[3072,512]{0,1:T(8,128)(2,1)}, bf16[3072,512]{0,1:T(8,128)(2,1)S(1)}, u32[]{:S(2)}) copy-start(bf16[3072,512]{0,1:T(8,128)(2,1)S(1)} %pad_maximum_fusion.12) | copy-start | bytes 9437188 | tf_op jit(solution)/shard_map/while
  861.1 28.4 %copy-start.9 = (bf16[3072,512]{0,1:T(8,128)(2,1)S(1)}, bf16[3072,512]{0,1:T(8,128)(2,1)}, u32[]{:S(2)}) copy-start(bf16[3072,512]{0,1:T(8,128)(2,1)} %copy-done.8) | copy-start | bytes 9437188 | tf_op jit(solution)/shard_map/while
  900.1 17.9 %copy-start.10 = (bf16[4,128,512]{2,1,0:T(8,128)(2,1)S(1)}, bf16[4,128,512]{2,1,0:T(8,128)(2,1)}, u32[]{:S(2)}) copy-start(bf16[4,128,512]{2,1,0:T(8,128)(2,1)} %fusion.137) | copy-start | bytes 1572868 | tf_op jit(solution)/shard_map/while
  955.9 97.1 %all-to-all-start.6 = ((bf16[8,256,512]{2,1,0:T(8,128)(2,1)}), bf16[8,256,512]{2,1,0:T(8,128)(2,1)S(1)}, u32[]{:S(2)}, u32[]{:S(2)}) async-start(bf16[8,256,512]{2,1,0:T(8,128)(2,1)} %bitcast.228), calls=%async_computation.6 | async-start | bytes 4194304 | tf_op jit(solution)/shard_map/all_to_all | solution.py:135
  963.0 41.5 %collective-permute-start.4 = (bf16[256,512]{1,0:T(8,128)(2,1)S(1)}, bf16[256,512]{1,0:T(8,128)(2,1)S(1)}, u32[]{:S(2)}, u32[]{:S(2)}) collective-permute-start(bf16[256,512]{1,0:T(8,128)(2,1)S(1)} %get-tuple-element.295), channel_id=1, source_target_pairs={{0,1},{1,2},{2,3},{3,4},{4,5},{5,6},{6,7},{7,0},{8,9},{9,10},{10,1... | collective-permute-start | bytes 786440 | tf_op jit(solution)/shard_map/ppermute | solution.py:27
  963.5 42.2 %collective-permute-start.5 = (bf16[256,512]{1,0:T(8,128)(2,1)S(1)}, bf16[256,512]{1,0:T(8,128)(2,1)S(1)}, u32[]{:S(2)}, u32[]{:S(2)}) collective-permute-start(bf16[256,512]{1,0:T(8,128)(2,1)S(1)} %get-tuple-element.294), channel_id=1, source_target_pairs={{0,2},{1,3},{2,4},{3,5},{4,6},{5,7},{6,0},{7,1},{8,10},{9,11},{10,... | collective-permute-start | bytes 786440 | tf_op jit(solution)/shard_map/ppermute | solution.py:27
  965.2 72.0 %collective-permute-start.6 = (bf16[256,512]{1,0:T(8,128)(2,1)S(1)}, bf16[256,512]{1,0:T(8,128)(2,1)S(1)}, u32[]{:S(2)}, u32[]{:S(2)}) collective-permute-start(bf16[256,512]{1,0:T(8,128)(2,1)S(1)} %get-tuple-element.293), channel_id=1, source_target_pairs={{0,3},{1,4},{2,5},{3,6},{4,7},{5,0},{6,1},{7,2},{8,11},{9,12},{10,... | collective-permute-start | bytes 786440 | tf_op jit(solution)/shard_map/ppermute | solution.py:27
  967.4 71.0 %collective-permute-start.7 = (bf16[256,512]{1,0:T(8,128)(2,1)S(1)}, bf16[256,512]{1,0:T(8,128)(2,1)S(1)}, u32[]{:S(2)}, u32[]{:S(2)}) collective-permute-start(bf16[256,512]{1,0:T(8,128)(2,1)S(1)} %get-tuple-element.292), channel_id=1, source_target_pairs={{0,4},{1,5},{2,6},{3,7},{4,0},{5,1},{6,2},{7,3},{8,12},{9,13},{10,... | collective-permute-start | bytes 786440 | tf_op jit(solution)/shard_map/ppermute | solution.py:27
  968.9 70.3 %collective-permute-start.8 = (bf16[256,512]{1,0:T(8,128)(2,1)S(1)}, bf16[256,512]{1,0:T(8,128)(2,1)S(1)}, u32[]{:S(2)}, u32[]{:S(2)}) collective-permute-start(bf16[256,512]{1,0:T(8,128)(2,1)S(1)} %get-tuple-element.291), channel_id=1, source_target_pairs={{0,5},{1,6},{2,7},{3,0},{4,1},{5,2},{6,3},{7,4},{8,13},{9,14},{10,... | collective-permute-start | bytes 786440 | tf_op jit(solution)/shard_map/ppermute | solution.py:27
  1004.5 35.4 %collective-permute-start.9 = (bf16[256,512]{1,0:T(8,128)(2,1)S(1)}, bf16[256,512]{1,0:T(8,128)(2,1)S(1)}, u32[]{:S(2)}, u32[]{:S(2)}) collective-permute-start(bf16[256,512]{1,0:T(8,128)(2,1)S(1)} %get-tuple-element.290), channel_id=1, source_target_pairs={{0,6},{1,7},{2,0},{3,1},{4,2},{5,3},{6,4},{7,5},{8,14},{9,15},{10,... | collective-permute-start | bytes 786440 | tf_op jit(solution)/shard_map/ppermute | solution.py:27
  1005.6 35.0 %collective-permute-start.10 = (bf16[256,512]{1,0:T(8,128)(2,1)S(1)}, bf16[256,512]{1,0:T(8,128)(2,1)S(1)}, u32[]{:S(2)}, u32[]{:S(2)}) collective-permute-start(bf16[256,512]{1,0:T(8,128)(2,1)S(1)} %get-tuple-element.289), channel_id=1, source_target_pairs={{0,7},{1,0},{2,1},{3,2},{4,3},{5,4},{6,5},{7,6},{8,15},{9,8},{10,9... | collective-permute-start | bytes 786440 | tf_op jit(solution)/shard_map/ppermute | solution.py:27
  (16 other events, 132.5 us)
Sparse Core Ops, SparseCore 0:
  956.0 70.2 reduce-scatter.1
